TPU v7x, 32 devices: a whole 2x2x4 slice. The times are simulated.
32 devices in a mesh: rows: 16 (over z, y, x), grp: 2 (over core).
Axes of the slice: x: 2, y: 2, z: 4, core: 2. Of those that a mesh axis runs over, the one named last changes fastest.
Arguments:
- perturb: bfloat16 [32768, 2040], P(('rows', 'grp')), may hold values from -6 to 6
- start_block: bfloat16 [2040, 128], replicated, may hold values from -6 to 6
Outputs:
- eofs: float32 [32768, 128], P(('rows', 'grp'))
- loadings: float32 [2040, 128], P('grp')
All inputs are finite; a program needn't handle non-finite values.
Results may differ from a plain program's by a relative error of at most 0.009.
Values may be sent and summed in bfloat16 or wider, within the bound.
A program may use at most 64 MiB of HBM per device.

v0:
```python
import math

import jax
import jax.numpy as jnp
from jax import lax
from jax.sharding import PartitionSpec as P

ITERS = 2


def right_solve(factor, block):
    return jax.scipy.linalg.solve_triangular(factor, block.T, lower=True).T


def on_device(perturb, start_block):
    columns = perturb.shape[1]
    total_rows = perturb.shape[0] * lax.axis_size("rows") * lax.axis_size("grp")
    slab_rows = columns // lax.axis_size("grp")
    slab_start = lax.axis_index("grp") * slab_rows
    projected = jnp.dot(perturb, start_block, preferred_element_type=jnp.float32).astype(
        jnp.bfloat16
    )
    for sweep in range(ITERS):
        if sweep > 0:
            projected = jnp.dot(perturb, basis_in, preferred_element_type=jnp.float32).astype(
                jnp.bfloat16
            )
        gram_sum = jnp.dot(projected.T, projected, preferred_element_type=jnp.float32)
        panel_sum = jnp.dot(perturb.T, projected, preferred_element_type=jnp.float32)
        gram_sum, panel_sum = lax.psum((gram_sum, panel_sum), ("rows", "grp"))
        factor = jnp.linalg.cholesky(gram_sum)
        weights = right_solve(factor, panel_sum)
        basis_in = weights.astype(jnp.bfloat16)
        own_rows = lax.dynamic_slice_in_dim(weights, slab_start, slab_rows, 0)
    eofs = right_solve(factor, projected.astype(jnp.float32)) * math.sqrt(total_rows)
    loadings = own_rows * math.sqrt(columns / total_rows)
    return (eofs, loadings)


def solution(mesh):
    return jax.shard_map(
        on_device,
        mesh=mesh,
        in_specs=(P(("rows", "grp"), None), P()),
        out_specs=(P(("rows", "grp"), None), P("grp", None)),
        check_vma=False,
    )
```

profile of v0, /device:TPU:0, one launch (start us, length us, event | category | flops | bytes accessed | tf_op | source)
XLA Modules:
  0.0 350.6 jit_solution(15223992333317979327)
XLA Ops:
  7.2 0.0 copy-start
  7.2 0.0 all-reduce.7.cloned.1.call-start
  7.2 1.0 copy-done
  8.2 0.0 copy-start.1
  8.2 3.8 %convolution_convert_fusion.1 = bf16[1024,128]{1,0:T(8,128)(2,1)S(1)} fusion(bf16[1024,2040]{0,1:T(8,128)(2,1)} %param.5, bf16[2040,128]{1,0:T(8,128)(2,1)S(1)} %copy-done), kind=kOutput, calls=%fused_computation.2 | convolution fusion | flops 534904832 | bytes 4962304 | tf_op jit(solution)/shard_map/dot_general | solution.py:20
  12.0 0.0 copy-done.1
  12.0 2.5 fusion.9
  14.5 0.9 fusion.8
  15.4 0.0 all-reduce.7.cloned.1.call-update
  15.4 0.2 all-reduce.5.cloned.1.call-start
  15.7 133.7 %all-reduce.7.cloned.1.call-done = (f32[128,2040]{1,0:T(8,128)}, f32[128,128]{0,1:T(8,128)}) async-done(((f32[128,2040]{1,0:T(8,128)}, f32[128,128]{0,1:T(8,128)}), (f32[128,2040]{1,0:T(8,128)}, f32[128,128]{0,1:T(8,128)})) %all-reduce.7.cloned.1.call-update) | async-done | bytes 1110032 | tf_op jit(solution)/shard_map/psum | solution.py:30
  149.4 0.9 copy.5
  150.4 0.9 fusion.7
  151.2 11.7 %cholesky.44 = f32[128,128]{1,0:T(8,128)S(1)} custom-call(f32[128,128]{1,0:T(8,128)S(1)} %fusion.7), custom_call_target="Cholesky" | custom-call | tf_op jit(solution)/shard_map/jit(cholesky)/cholesky | solution.py:31
  163.0 0.6 compare_reduce_fusion.1
  163.6 0.7 fusion
  164.3 9.8 %custom-call.11 = f32[1,128,128]{1,2,0:T(8,128)S(1)} custom-call(f32[1,128,128]{2,1,0:T(8,128)S(1)} %fusion), custom_call_target="InvertDiagBlocksLowerTriangular" | custom-call | tf_op jit(solution)/shard_map/jit(_solve_triangular)/triangular_solve | solution.py:12
  174.1 0.0 copy-start.2
  174.1 2.4 convolution_convert_fusion
  176.5 3.1 convolution_convert_fusion.2
  179.6 0.0 copy-done.2
  179.6 2.5 fusion.11
  182.2 0.9 fusion.10
  183.0 0.0 all-reduce.5.cloned.1.call-update
  183.1 131.1 %all-reduce.5.cloned.1.call-done = (f32[128,128]{0,1:T(8,128)}, f32[128,2040]{1,0:T(8,128)}) async-done(((f32[128,128]{0,1:T(8,128)}, f32[128,2040]{1,0:T(8,128)}), (f32[128,128]{0,1:T(8,128)}, f32[128,2040]{1,0:T(8,128)})) %all-reduce.5.cloned.1.call-update) | async-done | bytes 1110032 | tf_op jit(solution)/shard_map/psum | solution.py:30
  314.2 0.9 copy.7
  315.1 0.9 fusion.5
  315.9 11.9 %cholesky.55 = f32[128,128]{1,0:T(8,128)S(1)} custom-call(f32[128,128]{1,0:T(8,128)S(1)} %fusion.5), custom_call_target="Cholesky" | custom-call | tf_op jit(solution)/shard_map/jit(cholesky)/cholesky | solution.py:31
  327.9 0.6 compare_reduce_fusion
  328.5 0.7 fusion.1
  329.2 9.8 %custom-call.9 = f32[1,128,128]{1,2,0:T(8,128)S(1)} custom-call(f32[1,128,128]{2,1,0:T(8,128)S(1)} %fusion.1), custom_call_target="InvertDiagBlocksLowerTriangular" | custom-call | tf_op jit(solution)/shard_map/jit(_solve_triangular)/triangular_solve | solution.py:12
  339.0 1.2 convolution_multiply_fusion
  340.3 2.3 fusion.2
  342.5 0.2 multiply_bitcast_fusion
  342.7 1.0 copy.8
  (2 shorter events, 0.1 us)
Async XLA Ops:
  7.2 1.0 copy-start
  7.2 142.2 %all-reduce.7.cloned.1.call-start = ((), (), s32[]{:S(2)}) async-start(), calls=%async_computation.1 | async-start | bytes 2228224 | tf_op jit(solution)/shard_map/psum | solution.py:30
  8.2 3.8 %copy-start.1 = (bf16[1024,2040]{0,1:T(8,128)(2,1)S(1)}, bf16[1024,2040]{0,1:T(8,128)(2,1)}, u32[]{:S(2)}) copy-start(bf16[1024,2040]{0,1:T(8,128)(2,1)} %param.5) | copy-start | bytes 12533764
  15.4 298.7 %all-reduce.5.cloned.1.call-start = ((), (), s32[]{:S(2)}) async-start(), calls=%async_computation | async-start | bytes 2228224 | tf_op jit(solution)/shard_map/psum | solution.py:30
  174.1 5.5 %copy-start.2 = (bf16[1024,2040]{0,1:T(8,128)(2,1)S(1)}, bf16[1024,2040]{0,1:T(8,128)(2,1)}, u32[]{:S(2)}) copy-start(bf16[1024,2040]{0,1:T(8,128)(2,1)} %param.5) | copy-start | bytes 12533764
Sparse Core Ops, SparseCore 0:
  15.6 133.8 all-reduce.6
  183.2 130.9 all-reduce.4
where the time goes:
time: 351 us
  waiting for transfers between devices  265 us (75%)
  other arithmetic  47.8 us (14%)
  matrix products  19.6 us (6%)
  between operations  14.2 us (4%)
  local copies, waits for them, and re-layouts  3.85 us (1%)
    psum x2, waiting for transfers between devices, on_device(): gram_sum, panel_sum = lax.psum((gram_sum, panel_sum), ('rows', 'grp'))  265 us
    another operation x6, other arithmetic, on_device(): factor = jnp.linalg.cholesky(gram_sum)  25 us
    another operation x4, other arithmetic, right_solve(): return jax.scipy.linalg.solve_triangular(factor, block.T, lower=True).T  20.9 us
  transfers between devices with their start and end apart: 2, of which 2 were waited for; matrix products, arithmetic and copies ran while one was open for 0% of the time, Pallas kernels for 0%

commit v1 on v0

v1 whole, which is shorter than its diff:
```python
import functools
import math

import jax
import jax.numpy as jnp
from jax import lax
from jax.experimental import pallas as pl
from jax.experimental.pallas import tpu as pltpu
from jax.sharding import PartitionSpec as P

ITERS = 2
LANES = 128
F32 = jnp.float32
BF16 = jnp.bfloat16
MESH = pl.DeviceIdType.MESH


def round_up(value, unit):
    return (value + unit - 1) // unit * unit


def each(start, stop, body):
    if stop - start <= 16:
        for index in range(start, stop):
            body(index)
    else:
        @pl.loop(start, stop)
        def _(index):
            body(index)


def nt_dot(a, b, **kw):
    return lax.dot_general(a, b, (((1,), (1,)), ((), ())), preferred_element_type=F32, **kw)


def tn_dot(a, b, **kw):
    return lax.dot_general(a, b, (((0,), (0,)), ((), ())), preferred_element_type=F32, **kw)


def inverse_factor(work, inverse):
    rank = inverse.shape[0]
    size = 8
    row = lax.broadcasted_iota(jnp.int32, (rank, rank), 0)
    column = lax.broadcasted_iota(jnp.int32, (rank, rank), 1)
    work[:, rank:] = (row == column).astype(F32)
    sublane = lax.broadcasted_iota(jnp.int32, (size, 2 * rank), 0)
    for at in range(0, rank, size):
        rows = work[at : at + size, :]
        columns = [
            jnp.broadcast_to(rows[:, at + k : at + k + 1], (size, rank)) for k in range(size)
        ]
        d = {
            (i, k): jnp.broadcast_to(columns[k][i : i + 1, :], (size, rank))
            for k in range(size)
            for i in range(k, size)
        }
        held = [
            [
                jnp.broadcast_to(rows[i : i + 1, h * rank : (h + 1) * rank], (size, rank))
                for h in range(2)
            ]
            for i in range(size)
        ]
        for k in range(size):
            scale = lax.rsqrt(d[k, k])
            held[k] = [part * scale for part in held[k]]
            low = {i: d[i, k] * scale for i in range(k + 1, size)}
            for j in range(k + 1, size):
                for i in range(j, size):
                    d[i, j] = d[i, j] - low[i] * low[j]
                held[j] = [held[j][h] - low[j] * held[k][h] for h in range(2)]
        block = jnp.concatenate(held[0], axis=1)
        for k in range(1, size):
            block = jnp.where(sublane == k, jnp.concatenate(held[k], axis=1), block)
        inverse[at : at + size, :] = block[:, rank:]
        if at + size < rank:
            first = block.astype(BF16).astype(F32)
            rest = block - first
            second = rest.astype(BF16).astype(F32)
            third = rest - second
            left = jnp.concatenate([first, first, second, first, third, second], axis=0)
            right = jnp.concatenate([first, second, first, third, first, second], axis=0)
            update = tn_dot(left[:, :rank].astype(BF16), right.astype(BF16))
            work[at + size :, :] = work[at + size :, :] - update[at + size :, :]


def kernel(
    nr, ng, wire,
    perturb, start_block, eofs, loadings_t,
    proj, gram, gpair, gchunk, gfull, panel, ppair, pchunk, pfull, basis, work, inverse,
    s_g0, r_g0, s_g1, r_g1, s_g2, r_g2, s_p0, r_p0, s_p1, r_p1, s_p2, r_p2, s_p3, r_p3, s_p4, r_p4,
):
    r, g = lax.axis_index("rows"), lax.axis_index("grp")
    rows, columns = perturb.shape
    rank = start_block.shape[1]
    padded = panel.shape[2]
    part = rank // ng
    piece = gchunk.shape[2]
    row_tile = math.gcd(rows, 256)

    def row_peer(o):
        return lax.rem(r + o, nr)

    def grp_peer(o):
        return lax.rem(g + o, ng)

    barrier = pltpu.get_barrier_semaphore()

    def greet_row(o):
        pl.semaphore_signal(barrier, inc=1, device_id=(row_peer(o), g), device_id_type=MESH)

    def greet_grp(o):
        pl.semaphore_signal(barrier, inc=1, device_id=(r, grp_peer(o)), device_id_type=MESH)

    each(1, nr, greet_row)
    each(1, ng, greet_grp)

    def remote(src, dst, send, recv, device):
        return pltpu.make_async_remote_copy(
            src_ref=src, dst_ref=dst, send_sem=send, recv_sem=recv,
            device_id=device, device_id_type=MESH,
        )

    own_rank = pl.ds(pl.multiple_of(g * part, part), part)
    own_columns = pl.ds(pl.multiple_of(r * LANES, LANES), LANES)

    def lanes_of(index):
        return pl.ds(pl.multiple_of(index * LANES, LANES), LANES)

    def pieces_of(index):
        return pl.ds(pl.multiple_of(index * piece, piece), piece)

    for it in range(ITERS):
        for at in range(0, rows, row_tile):
            tile = perturb[at : at + row_tile, :]
            if it == 0:
                product = jnp.dot(tile, start_block[...], preferred_element_type=F32)
            else:
                product = nt_dot(tile, basis[it - 1, :, :columns])
            proj[at : at + row_tile, :] = product.astype(BF16)
        proj_t = proj[...].T
        gpair[it, g] = nt_dot(proj_t, proj_t)
        if it == 0:
            pl.semaphore_wait(barrier, nr - 1 + ng - 1)

        def g0(o):
            return remote(gpair.at[it, g], gpair.at[it, g], s_g0.at[it, o], r_g0.at[it, o], (r, grp_peer(o)))

        def g1(o):
            return remote(
                gram.at[it, pieces_of(row_peer(o))], gchunk.at[it, r],
                s_g1.at[it, o], r_g1.at[it, o], (row_peer(o), g),
            )

        def g2(o):
            return remote(
                gfull.at[it, pieces_of(r)], gfull.at[it, pieces_of(r)],
                s_g2.at[it, o], r_g2.at[it, o], (row_peer(o), g),
            )

        def p0(o):
            there = pl.ds(pl.multiple_of(grp_peer(o) * part, part), part)
            return remote(panel.at[it, there], ppair.at[it, g], s_p0.at[it, o], r_p0.at[it, o], (r, grp_peer(o)))

        def p1(o):
            return remote(
                ppair.at[it, g, :, lanes_of(row_peer(o))], pchunk.at[it, r],
                s_p1.at[it, o], r_p1.at[it, o], (row_peer(o), g),
            )

        def p2(o):
            return remote(pfull.at[it, own_rank], pfull.at[it, own_rank], s_p2.at[it, o], r_p2.at[it, o], (r, grp_peer(o)))

        def p3(o):
            block = basis.at[it, own_rank, own_columns]
            return remote(block, block, s_p3.at[it, o], r_p3.at[it, o], (row_peer(o), g))

        def p4(o, q):
            block = basis.at[it, own_rank, lanes_of(lax.rem(r + nr - o, nr))]
            return remote(block, block, s_p4.at[it, o, q], r_p4.at[it, o, q], (r, grp_peer(q)))

        each(1, ng, lambda o: g0(o).start())
        steps = [(at, min(at + 512, columns)) for at in range(0, columns, 512)]

        def panel_steps(chosen):
            for at, to in chosen:
                panel[it, :, at:to] = jnp.dot(proj_t, perturb[:, at:to], preferred_element_type=F32)

        if padded > columns:
            floor = columns // LANES * LANES
            panel[it, :, floor:] = jnp.zeros((rank, padded - floor), F32)
        panel_steps(steps[:1])
        each(1, ng, lambda o: g0(o).wait())
        total = gpair[it, 0]
        for index in range(1, ng):
            total = total + gpair[it, index]
        gram[it, :rank] = total
        each(1, nr, lambda o: g1(o).start())
        gchunk[it, r] = gram[it, pieces_of(r)]
        panel_steps(steps[1:])
        each(1, ng, lambda o: p0(o).start())
        ppair[it, g] = panel[it, own_rank]
        each(1, nr, lambda o: g1(o).wait())
        gfull[it, pieces_of(r)] = jnp.sum(gchunk[it], axis=0)
        each(1, nr, lambda o: g2(o).start())
        each(1, ng, lambda o: p0(o).wait())
        total = ppair[it, 0]
        for index in range(1, ng):
            total = total + ppair[it, index]
        ppair[it, g] = total
        each(1, nr, lambda o: g2(o).wait())
        each(1, nr, lambda o: p1(o).start())
        pchunk[it, r] = ppair[it, g, :, own_columns]
        work[:, :rank] = gfull[it, :rank]
        inverse_factor(work, inverse)
        each(1, nr, lambda o: p1(o).wait())
        pfull[it, own_rank] = jnp.sum(pchunk[it], axis=0)
        each(1, ng, lambda o: p2(o).start())
        each(1, ng, lambda o: p2(o).wait())
        weights = jnp.dot(
            inverse[own_rank, :], pfull[it], precision=lax.Precision.HIGHEST, preferred_element_type=F32
        )
        basis[it, own_rank, own_columns] = weights.astype(BF16)
        each(1, nr, lambda o: p3(o).start())
        each(1, ng, lambda q: p4(0, q).start())
        if it == ITERS - 1:
            for at in range(0, rows, row_tile):
                eofs[at : at + row_tile, :] = nt_dot(
                    proj[at : at + row_tile, :].astype(F32), inverse[...], precision=lax.Precision.HIGHEST
                )

        def forward(o):
            p3(o).wait()
            each(1, ng, lambda q: p4(o, q).start())

        each(1, nr, forward)
        each(0, nr, lambda o: each(1, ng, lambda q: p4(o, q).wait()))
    loadings_t[...] = basis[ITERS - 1, :, :columns]


def on_device(perturb, start_block, *, nr, ng):
    rows, columns = perturb.shape
    rank = start_block.shape[1]
    total_rows = rows * nr * ng
    slab = columns // ng
    padded = max(LANES * nr, round_up(columns, LANES))
    piece = round_up(-(-rank // nr), 8)
    part = rank // ng
    dma = pltpu.SemaphoreType.DMA
    sems = []
    for n in (ng, nr, nr, ng, nr, ng, nr):
        sems += [dma((ITERS, n))] * 2
    sems += [dma((ITERS, nr, ng))] * 2
    vmem = pl.BlockSpec(memory_space=pltpu.VMEM)
    eofs, loadings_t = pl.pallas_call(
        functools.partial(kernel, nr, ng, F32),
        out_shape=(
            jax.ShapeDtypeStruct((rows, rank), F32),
            jax.ShapeDtypeStruct((rank, columns), BF16),
        ),
        in_specs=[vmem, vmem],
        out_specs=(vmem, vmem),
        scratch_shapes=[
            pltpu.VMEM((rows, rank), BF16),
            pltpu.VMEM((ITERS, piece * nr, rank), F32),
            pltpu.VMEM((ITERS, ng, rank, rank), F32),
            pltpu.VMEM((ITERS, nr, piece, rank), F32),
            pltpu.VMEM((ITERS, piece * nr, rank), F32),
            pltpu.VMEM((ITERS, rank, padded), F32),
            pltpu.VMEM((ITERS, ng, part, padded), F32),
            pltpu.VMEM((ITERS, nr, part, LANES), F32),
            pltpu.VMEM((ITERS, rank, LANES), F32),
            pltpu.VMEM((ITERS, rank, padded), BF16),
            pltpu.VMEM((rank, 2 * rank), F32),
            pltpu.VMEM((rank, rank), F32),
        ] + sems,
        compiler_params=pltpu.CompilerParams(
            collective_id=0, has_side_effects=True, vmem_limit_bytes=60 * 1024 * 1024
        ),
    )(perturb, start_block)
    own = lax.dynamic_slice_in_dim(loadings_t, lax.axis_index("grp") * slab, slab, 1).astype(F32).T
    return eofs * math.sqrt(total_rows), own * math.sqrt(columns / total_rows)


def solution(mesh):
    return jax.shard_map(
        functools.partial(on_device, nr=mesh.shape["rows"], ng=mesh.shape["grp"]),
        mesh=mesh,
        in_specs=(P(("rows", "grp"), None), P()),
        out_specs=(P(("rows", "grp"), None), P("grp", None)),
        check_vma=False,
    )
```

time: 351 us -> 90.4 us (0.26)
  waiting for transfers between devices: 265 us -> 0 us
  Pallas kernels: 0 us -> 78 us
  other arithmetic: 47.8 us -> 2.98 us
  matrix products: 19.6 us -> 0 us
  between operations: 14.2 us -> 0.65 us
  local copies, waits for them, and re-layouts: 3.85 us -> 7.54 us
    psum x2 -> x0, waiting for transfers between devices: 265 us -> none  [on_device(): gram_sum, panel_sum = lax.psum((gram_sum, panel_sum), ('rows', 'grp'))]
    pallas_call x0 -> x1, Pallas kernels: none -> 78 us  [on_device(): pl.pallas_call(functools.partial(kernel, nr, ng, F32), out_shape=(jax.Sha...]
    another operation x10 -> x0, other arithmetic: 45.9 us -> none  [the longest x6 25 us: on_device(): factor = jnp.linalg.cholesky(gram_sum)]
    dot_general x6 -> x0, matrix products: 13.7 us -> none  [the longest x2 5.08 us: on_device(): jnp.dot(perturb.T, projected, preferred_element_type=jnp.float32)]
    another operation x3 -> x0, matrix products: 5.89 us -> none  [right_solve(): return jax.scipy.linalg.solve_triangular(factor, block.T, lower=True).T]
    unnamed x7 -> x2, local copies, waits for them, and re-layouts: 2 us -> 7.54 us
  transfers between devices with their start and end apart: 2 -> 0, of which waited for: 2 -> 0; matrix products, arithmetic and copies ran while one was open for 0% -> 0% of each run, Pallas kernels for 0% -> 0%
where the time goes in v1:
time: 90.4 us; the launch traced here: 89.2 us
  Pallas kernels  78 us (86%)
  local copies, waits for them, and re-layouts  7.54 us (8%)
  other arithmetic  2.98 us (3%)
    pallas_call x1, Pallas kernels, on_device(): pl.pallas_call(functools.partial(kernel, nr, ng, F32), out_shape=(jax.Sha...  78 us
    unnamed x2, local copies, waits for them, and re-layouts  7.54 us
    mul x2, other arithmetic, on_device(): return (eofs * math.sqrt(total_rows), own * math.sqrt(columns / total_rows))  2.98 us

profile of v1, /device:TPU:0, one launch (start us, length us, event | category | flops | bytes accessed | tf_op | source)
XLA Modules:
  0.0 89.2 jit_solution(4249514281651706787)
XLA Ops:
  0.6 6.5 %copy.4.perturb = bf16[1024,2040]{1,0:T(8,128)(2,1)} copy(bf16[1024,2040]{0,1:T(8,128)(2,1)} %param.2) | data formatting | bytes 8355840 | tf_op args[0]
  7.2 78.0 %shard_map.41 = (f32[1024,128]{1,0:T(8,128)}, bf16[128,2040]{1,0:T(8,128)(2,1)}) custom-call(bf16[1024,2040]{1,0:T(8,128)(2,1)} %copy.4.perturb, bf16[2040,128]{1,0:T(8,128)(2,1)} %start_block.1), custom_call_target="tpu_custom_call" | custom-call | tf_op jit(solution)/shard_map/pallas_call | solution.py:255
  85.2 1.9 %broadcast_multiply_fusion = f32[1024,128]{1,0:T(8,128)} fusion(f32[1024,128]{1,0:T(8,128)} %get-tuple-element.4), kind=kLoop, calls=%fused_computation.1 | loop fusion | flops 131072 | bytes 1048576 | tf_op jit(solution)/shard_map/mul | solution.py:282
  87.1 1.1 %multiply_bitcast_fusion = f32[1020,128]{0,1:T(8,128)S(1)} fusion(bf16[128,2040]{1,0:T(8,128)(2,1)} %get-tuple-element.5, s32[]{:T(128)S(6)} %select_n.3), kind=kLoop, calls=%fused_computation | loop fusion | flops 261120 | bytes 783364 | tf_op jit(solution)/shard_map/mul | solution.py:282
  88.2 1.0 %copy.5 = f32[1020,128]{1,0:T(8,128)} copy(f32[1020,128]{0,1:T(8,128)S(1)} %multiply_bitcast_fusion) | data formatting | bytes 1044480
